TPU v7x, 32 devices: a whole 2x2x4 slice. The times are simulated.
32 devices in a mesh: tp: 8 (over z, y), dp: 4 (over x, core).
Axes of the slice: x: 2, y: 2, z: 4, core: 2. Of those that a mesh axis runs over, the one named last changes fastest.
Arguments:
- tokens: bfloat16 [768, 4096], P(('dp', 'tp')), may hold values from -6 to 6
- hidden_grad: bfloat16 [768, 14336], P('dp', 'tp'), may hold values from -0.59765625 to 0.59765625
- gate_value: bfloat16 [768, 14336], P('dp', 'tp'), may hold values from -6 to 6
- up_value: bfloat16 [768, 14336], P('dp', 'tp'), may hold values from -6 to 6
- gate_weight: bfloat16 [4096, 14336], P('dp', 'tp'), may hold values from -0.09375 to 0.09375
- up_weight: bfloat16 [4096, 14336], P('dp', 'tp'), may hold values from -0.09375 to 0.09375
Outputs:
- input_grad: bfloat16 [768, 4096], P(('dp', 'tp'))
- gate_grad: bfloat16 [4096, 14336], P('dp', 'tp')
- up_grad: bfloat16 [4096, 14336], P('dp', 'tp')
All inputs are finite; a program needn't handle non-finite values.
Results may differ from a plain program's by a relative error of at most 0.018.
Values may be sent and summed in bfloat16 or wider, within the bound.
A program may use at most 128 MiB of HBM per device.

v0:
```python
import jax
import jax.numpy as jnp
from jax import lax
from jax.sharding import PartitionSpec as P


def on_device(tokens, hidden_grad, gate_value, up_value, gate_weight, up_weight):
    gathered = lax.all_gather(tokens, "tp", axis=0, tiled=True)
    gate_full, up_full = (
        lax.all_gather(gate_weight, "dp", axis=0, tiled=True),
        lax.all_gather(up_weight, "dp", axis=0, tiled=True),
    )
    gate_float = gate_value.astype(jnp.float32)
    up_float = up_value.astype(jnp.float32)
    logistic = jax.nn.sigmoid(gate_float)
    upstream = hidden_grad.astype(jnp.float32)
    d_gate = (upstream * up_float * logistic * (1.0 + gate_float * (1.0 - logistic))).astype(
        jnp.bfloat16
    )
    d_up = (upstream * gate_float * logistic).astype(jnp.bfloat16)
    across = (((1,), (1,)), ((), ()))
    contract = (((0,), (0,)), ((), ()))
    input_grad = lax.psum_scatter(
        (
            lax.dot_general(d_gate, gate_full, across, preferred_element_type=jnp.float32)
            + lax.dot_general(d_up, up_full, across, preferred_element_type=jnp.float32)
        ).astype(jnp.bfloat16),
        "tp",
        scatter_dimension=0,
        tiled=True,
    )
    grads_both = jnp.concatenate([d_gate, d_up], axis=1)
    hidden_width = d_gate.shape[1]
    group_rows = gathered.shape[0]
    columns = lax.all_to_all(gathered, "dp", split_axis=1, concat_axis=0, tiled=True)
    initial = jnp.zeros((gate_weight.shape[0], 2 * hidden_width), jnp.float32)
    pieces = lax.all_gather(grads_both, "dp", axis=0, tiled=True)
    group_count = pieces.shape[0] // group_rows

    def one_group(position, carried):
        within = position * group_rows
        grads_rows = lax.dynamic_slice_in_dim(pieces, within, group_rows, 0)
        block = lax.dynamic_slice_in_dim(columns, within, group_rows, 0)
        partial_value = lax.dot_general(
            block, grads_rows, contract, preferred_element_type=jnp.float32
        ).astype(jnp.bfloat16)
        partial_value = lax.optimization_barrier(partial_value)
        return carried + partial_value.astype(jnp.float32)

    summed = lax.fori_loop(0, group_count, one_group, initial)
    gate_grad = summed[:, :hidden_width].astype(jnp.bfloat16)
    up_grad = summed[:, hidden_width:].astype(jnp.bfloat16)
    return (input_grad, gate_grad, up_grad)


def solution(mesh):
    placed = (
        P(("dp", "tp"), None),
        P("dp", "tp"),
        P("dp", "tp"),
        P("dp", "tp"),
        P("dp", "tp"),
        P("dp", "tp"),
    )
    return jax.shard_map(
        on_device,
        mesh=mesh,
        in_specs=placed,
        out_specs=(P(("dp", "tp"), None), P("dp", "tp"), P("dp", "tp")),
        check_vma=False,
    )
```

profile of v0, /device:TPU:0, one launch (start us, length us, event | category | flops | bytes accessed | tf_op | source)
XLA Modules:
  0.0 376.7 jit_solution(9638341866954031148)
XLA Ops:
  7.2 0.0 all-gather.9.cloned.1.call-start
  7.2 0.7 all-gather.9.cloned.1.call-update
  7.9 0.0 copy-start
  7.9 0.0 copy-start.1
  7.9 0.0 all-gather.5.cloned.1.call-start
  8.0 0.7 all-gather.5.cloned.1.call-update
  8.7 0.0 all-gather.7.cloned.1.call-start
  8.7 0.7 all-gather.7.cloned.1.call-update
  9.4 0.0 all-gather.11.cloned.1.call-start
  9.4 0.0 copy-done
  9.5 0.0 copy-done.1
  9.5 1.8 fusion.12
  11.3 1.2 pad_maximum_fusion
  12.5 0.0 all-gather.11.cloned.1.call-update
  12.5 44.6 %all-gather.9.cloned.1.call-done = bf16[192,4096]{1,0:T(8,128)(2,1)} async-done(((bf16[24,4096]{1,0:T(8,128)(2,1)}), bf16[192,4096]{1,0:T(8,128)(2,1)}) %all-gather.9.cloned.1.call-update) | async-done | bytes 1572880 | tf_op jit(solution)/shard_map/all_gather | solution.py:8
  57.1 2.7 copy.12
  59.8 3.6 all-to-all-start
  63.4 0.0 reduce-scatter.2.cloned.1.call-start
  63.4 100.7 %all-gather.5.cloned.1.call-done = bf16[4096,1792]{1,0:T(8,128)(2,1)} async-done(((bf16[1024,1792]{1,0:T(8,128)(2,1)}), bf16[4096,1792]{1,0:T(8,128)(2,1)}) %all-gather.5.cloned.1.call-update) | async-done | bytes 14680080 | tf_op jit(solution)/shard_map/all_gather | solution.py:10
  164.1 11.9 %fusion.14 = f32[192,4096]{1,0:T(8,128)} fusion(bf16[192,1792]{1,0:T(8,128)(2,1)S(1)} %get-tuple-element.109, bf16[4096,1792]{1,0:T(8,128)(2,1)} %all-gather.5.cloned.1.call-done), kind=kOutput, calls=%fused_computation.23 | convolution fusion | flops 2818572288 | bytes 18513920 | tf_op jit(solution)/shard_map/dot_general | solution.py:25
  176.0 81.2 %all-gather.7.cloned.1.call-done = bf16[4096,1792]{1,0:T(8,128)(2,1)} async-done(((bf16[1024,1792]{1,0:T(8,128)(2,1)}), bf16[4096,1792]{1,0:T(8,128)(2,1)}) %all-gather.7.cloned.1.call-update) | async-done | bytes 14680080 | tf_op jit(solution)/shard_map/all_gather | solution.py:11
  257.1 12.1 %fusion.3 = bf16[192,4096]{1,0:T(8,128)(2,1)} fusion(f32[192,4096]{1,0:T(8,128)} %fusion.14, bf16[192,1792]{1,0:T(8,128)(2,1)S(1)} %get-tuple-element.108, bf16[4096,1792]{1,0:T(8,128)(2,1)} %all-gather.7.cloned.1.call-done), kind=kOutput, calls=%fused_computation.6 | convolution fusion | flops 2820145152 | bytes 20086784 | tf_op jit(solution)/shard_map/dot_general | solution.py:26
  269.3 0.0 reduce-scatter.2.cloned.1.call-update
  269.3 0.0 all-to-all-done
  269.3 31.2 %all-gather.11.cloned.1.call-done = bf16[768,3584]{1,0:T(8,128)(2,1)} async-done(((bf16[192,3584]{1,0:T(8,128)(2,1)}), bf16[768,3584]{1,0:T(8,128)(2,1)}) %all-gather.11.cloned.1.call-update) | async-done | bytes 5505040 | tf_op jit(solution)/shard_map/all_gather | solution.py:37
  300.5 52.8 %while.14 = (s32[]{:T(128)}, f32[1024,3584]{1,0:T(8,128)}, bf16[768,1024]{1,0:T(8,128)(2,1)S(1)}, bf16[768,3584]{1,0:T(8,128)(2,1)}, s32[]{:T(128)}, /*index=5*/s32[]{:T(128)}, s32[]{:T(128)}, s32[]{:T(128)}) while((s32[]{:T(128)}, f32[1024,3584]{1,0:T(8,128)}, bf16[768,1024]{1,0:T(8,128)(2,1)S(1)}, bf16[768,3584]{1,0:T(8,128)(2,1)}, ...), condition=%wide.region_2.0_spmd.clone, body=%wide.region_1.0_spmd.clone.sunk | while | flops 1423966208 | bytes 45810836 | solution.py:50
  300.5 3.5 convolution_convert_fusion.2
  304.0 5.9 %select_add_fusion.2 = f32[1024,3584]{1,0:T(8,128)} fusion(f32[1024,3584]{1,0:T(8,128)} %get-tuple-element.144, bf16[1024,3584]{1,0:T(8,128)(2,1)S(1)} %convolution_convert_fusion.2, pred[]{:T(512)S(6)} %compare.3), kind=kLoop, calls=%fused_computation.clone.1 | loop fusion | flops 11010048 | bytes 36700160 | tf_op jit(solution)/shard_map/while/body/eval_jaxpr/add | solution.py:48
  309.9 3.4 convolution_convert_fusion.2
  313.4 11.0 %select_add_fusion.2 = f32[1024,3584]{1,0:T(8,128)} fusion(f32[1024,3584]{1,0:T(8,128)} %get-tuple-element.144, bf16[1024,3584]{1,0:T(8,128)(2,1)S(1)} %convolution_convert_fusion.2, pred[]{:T(512)S(6)} %compare.3), kind=kLoop, calls=%fused_computation.clone.1 | loop fusion | flops 11010048 | bytes 36700160 | tf_op jit(solution)/shard_map/while/body/eval_jaxpr/add | solution.py:48
  324.4 3.5 convolution_convert_fusion.2
  327.9 11.0 %select_add_fusion.2 = f32[1024,3584]{1,0:T(8,128)} fusion(f32[1024,3584]{1,0:T(8,128)} %get-tuple-element.144, bf16[1024,3584]{1,0:T(8,128)(2,1)S(1)} %convolution_convert_fusion.2, pred[]{:T(512)S(6)} %compare.3), kind=kLoop, calls=%fused_computation.clone.1 | loop fusion | flops 11010048 | bytes 36700160 | tf_op jit(solution)/shard_map/while/body/eval_jaxpr/add | solution.py:48
  338.9 3.4 convolution_convert_fusion.2
  342.3 11.0 %select_add_fusion.2 = f32[1024,3584]{1,0:T(8,128)} fusion(f32[1024,3584]{1,0:T(8,128)} %get-tuple-element.144, bf16[1024,3584]{1,0:T(8,128)(2,1)S(1)} %convolution_convert_fusion.2, pred[]{:T(512)S(6)} %compare.3), kind=kLoop, calls=%fused_computation.clone.1 | loop fusion | flops 11010048 | bytes 36700160 | tf_op jit(solution)/shard_map/while/body/eval_jaxpr/add | solution.py:48
  353.3 9.1 %convert.4 = bf16[1024,3584]{1,0:T(8,128)(2,1)} convert(f32[1024,3584]{1,0:T(8,128)} %get-tuple-element.82) | non-fusion elementwise | flops 3670016 | bytes 22020096 | tf_op jit(solution)/shard_map/convert.1
  362.4 6.7 %fusion.13 = (bf16[1024,1792]{1,0:T(8,128)(2,1)}, bf16[1024,1792]{1,0:T(8,128)(2,1)}) fusion(bf16[1024,3584]{1,0:T(8,128)(2,1)} %convert.4), kind=kLoop, calls=%fused_computation.22 | loop fusion | bytes 14680064 | tf_op jit(solution)/shard_map/slice | solution.py:52
  369.1 1.0 reduce-scatter.2.cloned.1.call-done
  (1 shorter events, 0.0 us)
Async XLA Ops:
  7.2 49.9 %all-gather.9.cloned.1.call-start = ((), (), s32[]{:S(2)}) async-start(), calls=%async_computation.5 | async-start | bytes 1769472 | tf_op jit(solution)/shard_map/all_gather | solution.py:8
  7.9 1.6 copy-start
  7.9 1.6 copy-start.1
  7.9 156.2 %all-gather.5.cloned.1.call-start = ((), (), s32[]{:S(2)}) async-start(), calls=%async_computation.2 | async-start | bytes 18350080 | tf_op jit(solution)/shard_map/all_gather | solution.py:10
  8.7 248.5 %all-gather.7.cloned.1.call-start = ((), (), s32[]{:S(2)}) async-start(), calls=%async_computation.3 | async-start | bytes 18350080 | tf_op jit(solution)/shard_map/all_gather | solution.py:11
  9.4 291.1 %all-gather.11.cloned.1.call-start = ((), (), s32[]{:S(2)}) async-start(), calls=%async_computation.6 | async-start | bytes 6881280 | tf_op jit(solution)/shard_map/all_gather | solution.py:37
  59.8 209.5 %all-to-all-start = ((bf16[192,4,1024]{2,0,1:T(8,128)(2,1)}), bf16[192,4,1024]{2,0,1:T(8,128)(2,1)S(1)}, u32[]{:S(2)}, u32[]{:S(2)}) async-start(bf16[192,4,1024]{2,0,1:T(8,128)(2,1)} %bitcast.10), calls=%async_computation.1 | async-start | bytes 3145728 | tf_op jit(solution)/shard_map/all_to_all | solution.py:35
  63.4 306.8 %reduce-scatter.2.cloned.1.call-start = ((), (), s32[]{:S(2)}) async-start(), calls=%async_computation.4 | async-start | bytes 1769472 | tf_op jit(solution)/shard_map/reduce_scatter | solution.py:23
Sparse Core Ops, SparseCore 0:
  10.2 46.8 all-gather.8
  58.6 105.4 all-gather.4
  165.7 91.4 all-gather.6
  258.6 41.8 all-gather.10
  304.3 65.7 reduce-scatter.1
where the time goes:
time: 377 us
  waiting for transfers between devices  261 us (69%)
  other arithmetic  51.1 us (14%)
  matrix products  37.9 us (10%)
  between operations  13.8 us (4%)
  local copies, waits for them, and re-layouts  9.4 us (2%)
    all_gather x1, waiting for transfers between devices, on_device(): lax.all_gather(gate_weight, 'dp', axis=0, tiled=True)  101 us
    all_gather x1, waiting for transfers between devices, on_device(): lax.all_gather(up_weight, 'dp', axis=0, tiled=True)  81.2 us
    all_gather x1, waiting for transfers between devices, on_device(): gathered = lax.all_gather(tokens, 'tp', axis=0, tiled=True)  44.6 us
    add x4, other arithmetic, one_group(): return carried + partial_value.astype(jnp.float32)  39 us
    all_gather x1, waiting for transfers between devices, on_device(): pieces = lax.all_gather(grads_both, 'dp', axis=0, tiled=True)  31.2 us
    dot_general x4, matrix products, one_group(): lax.dot_general(block, grads_rows, contract, preferred_element_type=jnp.f...  13.8 us
    dot_general x1, matrix products, on_device(): lax.dot_general(d_up, up_full, across, preferred_element_type=jnp.float32)  12.1 us
    dot_general x1, matrix products, on_device(): lax.dot_general(d_gate, gate_full, across, preferred_element_type=jnp.flo...  11.9 us
  transfers between devices with their start and end apart: 6, of which 5 were waited for; matrix products, arithmetic and copies ran while one was open for 26% of the time, Pallas kernels for 0%

commit v1 on v0

--- a/solution.py
+++ b/solution.py
@@ -34,7 +34,12 @@
     group_rows = gathered.shape[0]
     columns = lax.all_to_all(gathered, "dp", split_axis=1, concat_axis=0, tiled=True)
     initial = jnp.zeros((gate_weight.shape[0], 2 * hidden_width), jnp.float32)
-    pieces = lax.all_gather(grads_both, "dp", axis=0, tiled=True)
+    ring = [grads_both]
+    for hop in range(3):
+        ring.append(lax.ppermute(ring[-1], "dp", [(dev, (dev + 1) % 4) for dev in range(4)]))
+    pieces = jnp.roll(
+        jnp.concatenate(ring[::-1], axis=0), (lax.axis_index("dp") + 1) * ring[0].shape[0], axis=0
+    )
     group_count = pieces.shape[0] // group_rows
 
     def one_group(position, carried):

time: 377 us -> 350 us (0.928)
  waiting for transfers between devices: 261 us -> 222 us
  local copies, waits for them, and re-layouts: 9.4 us -> 21.1 us
    ppermute x0 -> x3, waiting for transfers between devices: none -> 39.1 us  [on_device(): lax.ppermute(ring[-1], 'dp', [(dev, (dev + 1) % 4) for dev in range(4)])]
    all_gather x1, waiting for transfers between devices: 44.6 us -> 8.33 us  [on_device(): gathered = lax.all_gather(tokens, 'tp', axis=0, tiled=True)]
    all_gather x1 -> x0, waiting for transfers between devices: 31.2 us -> none  [on_device(): pieces = lax.all_gather(grads_both, 'dp', axis=0, tiled=True)]
    all_gather x1, waiting for transfers between devices: 101 us -> 86.7 us  [on_device(): lax.all_gather(gate_weight, 'dp', axis=0, tiled=True)]
    unnamed x4 -> x14, local copies, waits for them, and re-layouts: 0.01 us -> 7.95 us
    all_gather x1, waiting for transfers between devices: 81.2 us -> 85.9 us  [on_device(): lax.all_gather(up_weight, 'dp', axis=0, tiled=True)]
  transfers between devices with their start and end apart: 6 -> 8, of which waited for: 5 -> 6; matrix products, arithmetic and copies ran while one was open for 26% -> 31% of each run, Pallas kernels for 0% -> 0%
where the time goes in v1:
time: 350 us; the launch traced here: 349 us
  waiting for transfers between devices  222 us (63%)
  other arithmetic  49.8 us (14%)
  matrix products  37.7 us (11%)
  local copies, waits for them, and re-layouts  21.1 us (6%)
  between operations  13.9 us (4%)
  starting transfers between devices  4.27 us (1%)
    all_gather x1, waiting for transfers between devices, on_device(): lax.all_gather(gate_weight, 'dp', axis=0, tiled=True)  86.7 us
    all_gather x1, waiting for transfers between devices, on_device(): lax.all_gather(up_weight, 'dp', axis=0, tiled=True)  85.9 us
    ppermute x3, waiting for transfers between devices, on_device(): lax.ppermute(ring[-1], 'dp', [(dev, (dev + 1) % 4) for dev in range(4)])  39.1 us
    add x4, other arithmetic, one_group(): return carried + partial_value.astype(jnp.float32)  38.7 us
    dot_general x4, matrix products, one_group(): lax.dot_general(block, grads_rows, contract, preferred_element_type=jnp.f...  13.8 us
    dot_general x1, matrix products, on_device(): lax.dot_general(d_up, up_full, across, preferred_element_type=jnp.float32)  12.1 us
    dot_general x1, matrix products, on_device(): lax.dot_general(d_gate, gate_full, across, preferred_element_type=jnp.flo...  11.7 us
    another operation x1, other arithmetic  9.01 us
  transfers between devices with their start and end apart: 8, of which 6 were waited for; matrix products, arithmetic and copies ran while one was open for 31% of the time, Pallas kernels for 0%

profile of v1, /device:TPU:0, one launch (start us, length us, event | category | flops | bytes accessed | tf_op | source)
XLA Modules:
  0.0 348.9 jit_solution(5509503127290060144)
XLA Ops:
  7.2 0.0 all-gather.8.cloned.1.call-start
  7.2 0.7 all-gather.8.cloned.1.call-update
  7.9 0.0 copy-start.2
  7.9 0.0 copy-start.3
  7.9 0.0 all-gather.4.cloned.1.call-start
  8.0 0.7 all-gather.4.cloned.1.call-update
  8.7 0.0 all-gather.6.cloned.1.call-start
  8.7 0.7 all-gather.6.cloned.1.call-update
  9.4 1.8 fusion.12
  11.2 0.1 pad_maximum_fusion
  11.3 0.5 collective-permute-start
  11.9 17.9 %collective-permute-done = bf16[192,3584]{1,0:T(8,128)(2,1)S(1)} collective-permute-done((bf16[192,3584]{1,0:T(8,128)(2,1)S(1)}, bf16[192,3584]{1,0:T(8,128)(2,1)S(1)}, u32[]{:S(2)}, u32[]{:S(2)}) %collective-permute-start) | collective-permute-done | bytes 1376288 | tf_op jit(solution)/shard_map/ppermute | solution.py:39
  29.8 1.1 copy-done
  30.9 0.0 collective-permute-start.1
  30.9 17.8 %collective-permute-done.1 = bf16[192,3584]{1,0:T(8,128)(2,1)} collective-permute-done((bf16[192,3584]{1,0:T(8,128)(2,1)S(1)}, bf16[192,3584]{1,0:T(8,128)(2,1)}, u32[]{:S(2)}, u32[]{:S(2)}) %collective-permute-start.1) | collective-permute-done | bytes 1376288 | tf_op jit(solution)/shard_map/ppermute | solution.py:39
  48.7 0.0 collective-permute-start.2
  48.7 8.3 %all-gather.8.cloned.1.call-done = bf16[192,4096]{1,0:T(8,128)(2,1)} async-done(((bf16[24,4096]{1,0:T(8,128)(2,1)}), bf16[192,4096]{1,0:T(8,128)(2,1)}) %all-gather.8.cloned.1.call-update) | async-done | bytes 1572880 | tf_op jit(solution)/shard_map/all_gather | solution.py:8
  57.0 2.7 copy.12
  59.8 3.6 %all-to-all-start = ((bf16[192,4,1024]{2,0,1:T(8,128)(2,1)}), bf16[192,4,1024]{2,0,1:T(8,128)(2,1)S(1)}, u32[]{:S(2)}, u32[]{:S(2)}) async-start(bf16[192,4,1024]{2,0,1:T(8,128)(2,1)} %bitcast.12), calls=%async_computation.1 | async-start | bytes 3145728 | tf_op jit(solution)/shard_map/all_to_all | solution.py:35
  63.3 0.0 reduce-scatter.2.cloned.1.call-start
  63.4 0.0 copy-start.1
  63.4 3.4 collective-permute-done.2
  66.8 1.7 constant_dynamic-update-slice_fusion.7
  68.4 1.6 constant_dynamic-update-slice_fusion.6
  70.1 0.1 constant_dynamic-update-slice_fusion.5
  70.2 0.1 constant_dynamic-update-slice_fusion.4
  70.2 1.8 constant_dynamic-update-slice_fusion.3
  72.1 1.6 constant_dynamic-update-slice_fusion.2
  73.7 0.1 constant_dynamic-update-slice_fusion.1
  73.8 0.1 constant_dynamic-update-slice_fusion
  73.9 3.7 %constant_dynamic-slice_fusion = bf16[768,3584]{1,0:T(8,128)(2,1)} fusion(bf16[1536,3584]{1,0:T(8,128)(2,1)S(1)} %constant_dynamic-update-slice_fusion, s32[]{:T(128)S(6)} %select_n.22), kind=kLoop, calls=%fused_computation.30 | loop fusion | bytes 11010052 | tf_op jit(solution)/shard_map/jit(_roll_dynamic)/dynamic_slice | solution.py:40
  77.6 86.7 %all-gather.4.cloned.1.call-done = bf16[4096,1792]{1,0:T(8,128)(2,1)} async-done(((bf16[1024,1792]{1,0:T(8,128)(2,1)}), bf16[4096,1792]{1,0:T(8,128)(2,1)}) %all-gather.4.cloned.1.call-update) | async-done | bytes 14680080 | tf_op jit(solution)/shard_map/all_gather | solution.py:10
  164.2 11.7 %fusion.14 = f32[192,4096]{1,0:T(8,128)} fusion(bf16[192,1792]{1,0:T(8,128)(2,1)S(1)} %get-tuple-element.109, bf16[4096,1792]{1,0:T(8,128)(2,1)} %all-gather.4.cloned.1.call-done), kind=kOutput, calls=%fused_computation.32 | convolution fusion | flops 2818572288 | bytes 18513920 | tf_op jit(solution)/shard_map/dot_general | solution.py:25
  175.9 85.9 %all-gather.6.cloned.1.call-done = bf16[4096,1792]{1,0:T(8,128)(2,1)} async-done(((bf16[1024,1792]{1,0:T(8,128)(2,1)}), bf16[4096,1792]{1,0:T(8,128)(2,1)}) %all-gather.6.cloned.1.call-update) | async-done | bytes 14680080 | tf_op jit(solution)/shard_map/all_gather | solution.py:11
  261.9 12.1 %fusion.3 = bf16[192,4096]{1,0:T(8,128)(2,1)} fusion(f32[192,4096]{1,0:T(8,128)} %fusion.14, bf16[192,1792]{1,0:T(8,128)(2,1)S(1)} %get-tuple-element.108, bf16[4096,1792]{1,0:T(8,128)(2,1)} %all-gather.6.cloned.1.call-done), kind=kOutput, calls=%fused_computation.6 | convolution fusion | flops 2820145152 | bytes 20086784 | tf_op jit(solution)/shard_map/dot_general | solution.py:26
  274.0 0.0 reduce-scatter.2.cloned.1.call-update
  274.0 0.0 all-to-all-done
  274.0 52.6 %while.14 = (s32[]{:T(128)}, f32[1024,3584]{1,0:T(8,128)}, bf16[768,1024]{1,0:T(8,128)(2,1)S(1)}, bf16[768,3584]{1,0:T(8,128)(2,1)}, s32[]{:T(128)}, /*index=5*/s32[]{:T(128)}, s32[]{:T(128)}, s32[]{:T(128)}) while((s32[]{:T(128)}, f32[1024,3584]{1,0:T(8,128)}, bf16[768,1024]{1,0:T(8,128)(2,1)S(1)}, bf16[768,3584]{1,0:T(8,128)(2,1)}, ...), condition=%wide.region_2.3_spmd.clone, body=%wide.region_1.2_spmd.clone.sunk | while | flops 1423966208 | bytes 45810836 | solution.py:55
  274.0 3.5 convolution_convert_fusion.2
  277.5 5.9 %select_add_fusion.2 = f32[1024,3584]{1,0:T(8,128)} fusion(f32[1024,3584]{1,0:T(8,128)} %get-tuple-element.144, bf16[1024,3584]{1,0:T(8,128)(2,1)S(1)} %convolution_convert_fusion.2, pred[]{:T(512)S(6)} %compare.3), kind=kLoop, calls=%fused_computation.clone.1 | loop fusion | flops 11010048 | bytes 36700160 | tf_op jit(solution)/shard_map/while/body/eval_jaxpr/add | solution.py:53
  283.4 3.5 convolution_convert_fusion.2
  286.9 10.9 %select_add_fusion.2 = f32[1024,3584]{1,0:T(8,128)} fusion(f32[1024,3584]{1,0:T(8,128)} %get-tuple-element.144, bf16[1024,3584]{1,0:T(8,128)(2,1)S(1)} %convolution_convert_fusion.2, pred[]{:T(512)S(6)} %compare.3), kind=kLoop, calls=%fused_computation.clone.1 | loop fusion | flops 11010048 | bytes 36700160 | tf_op jit(solution)/shard_map/while/body/eval_jaxpr/add | solution.py:53
  297.8 3.5 convolution_convert_fusion.2
  301.2 11.0 %select_add_fusion.2 = f32[1024,3584]{1,0:T(8,128)} fusion(f32[1024,3584]{1,0:T(8,128)} %get-tuple-element.144, bf16[1024,3584]{1,0:T(8,128)(2,1)S(1)} %convolution_convert_fusion.2, pred[]{:T(512)S(6)} %compare.3), kind=kLoop, calls=%fused_computation.clone.1 | loop fusion | flops 11010048 | bytes 36700160 | tf_op jit(solution)/shard_map/while/body/eval_jaxpr/add | solution.py:53
  312.2 3.5 convolution_convert_fusion.2
  315.7 11.0 %select_add_fusion.2 = f32[1024,3584]{1,0:T(8,128)} fusion(f32[1024,3584]{1,0:T(8,128)} %get-tuple-element.144, bf16[1024,3584]{1,0:T(8,128)(2,1)S(1)} %convolution_convert_fusion.2, pred[]{:T(512)S(6)} %compare.3), kind=kLoop, calls=%fused_computation.clone.1 | loop fusion | flops 11010048 | bytes 36700160 | tf_op jit(solution)/shard_map/while/body/eval_jaxpr/add | solution.py:53
  326.6 9.0 %convert.4 = bf16[1024,3584]{1,0:T(8,128)(2,1)} convert(f32[1024,3584]{1,0:T(8,128)} %get-tuple-element.82) | non-fusion elementwise | flops 3670016 | bytes 22020096 | tf_op jit(solution)/shard_map/convert.1
  335.6 6.7 %fusion.13 = (bf16[1024,1792]{1,0:T(8,128)(2,1)}, bf16[1024,1792]{1,0:T(8,128)(2,1)}) fusion(bf16[1024,3584]{1,0:T(8,128)(2,1)} %convert.4), kind=kLoop, calls=%fused_computation.31 | loop fusion | bytes 14680064 | tf_op jit(solution)/shard_map/slice | solution.py:57
  (6 shorter events, 0.0 us)
Async XLA Ops:
  7.2 49.9 %all-gather.8.cloned.1.call-start = ((), (), s32[]{:S(2)}) async-start(), calls=%async_computation.5 | async-start | bytes 1769472 | tf_op jit(solution)/shard_map/all_gather | solution.py:8
  7.9 1.5 copy-start.2
  7.9 1.5 copy-start.3
  7.9 156.3 %all-gather.4.cloned.1.call-start = ((), (), s32[]{:S(2)}) async-start(), calls=%async_computation.2 | async-start | bytes 18350080 | tf_op jit(solution)/shard_map/all_gather | solution.py:10
  8.7 253.2 %all-gather.6.cloned.1.call-start = ((), (), s32[]{:S(2)}) async-start(), calls=%async_computation.3 | async-start | bytes 18350080 | tf_op jit(solution)/shard_map/all_gather | solution.py:11
  11.3 18.5 %collective-permute-start = (bf16[192,3584]{1,0:T(8,128)(2,1)S(1)}, bf16[192,3584]{1,0:T(8,128)(2,1)S(1)}, u32[]{:S(2)}, u32[]{:S(2)}) collective-permute-start(bf16[192,3584]{1,0:T(8,128)(2,1)S(1)} %pad_maximum_fusion), channel_id=1, source_target_pairs={{0,1},{1,2},{2,3},{3,0},{4,5},{5,6},{6,7},{7,4},{8,9},{9,10},{10,1... | collective-permute-start | bytes 4128776 | tf_op jit(solution)/shard_map/ppermute | solution.py:39
  29.8 1.1 copy-start
  30.9 17.8 %collective-permute-start.1 = (bf16[192,3584]{1,0:T(8,128)(2,1)S(1)}, bf16[192,3584]{1,0:T(8,128)(2,1)}, u32[]{:S(2)}, u32[]{:S(2)}) collective-permute-start(bf16[192,3584]{1,0:T(8,128)(2,1)S(1)} %collective-permute-done), channel_id=1, source_target_pairs={{0,1},{1,2},{2,3},{3,0},{4,5},{5,6},{6,7},{7,4},{8,9},{9,10},{10,1... | collective-permute-start | bytes 4128776 | tf_op jit(solution)/shard_map/ppermute | solution.py:39
  48.7 18.1 %collective-permute-start.2 = (bf16[192,3584]{1,0:T(8,128)(2,1)}, bf16[192,3584]{1,0:T(8,128)(2,1)}, u32[]{:S(2)}, u32[]{:S(2)}) collective-permute-start(bf16[192,3584]{1,0:T(8,128)(2,1)} %collective-permute-done.1), channel_id=1, source_target_pairs={{0,1},{1,2},{2,3},{3,0},{4,5},{5,6},{6,7},{7,4},{8,9},{9,10},{10,1... | collective-permute-start | bytes 4128776 | tf_op jit(solution)/shard_map/ppermute | solution.py:39
  59.8 214.3 %all-to-all-start = ((bf16[192,4,1024]{2,0,1:T(8,128)(2,1)}), bf16[192,4,1024]{2,0,1:T(8,128)(2,1)S(1)}, u32[]{:S(2)}, u32[]{:S(2)}) async-start(bf16[192,4,1024]{2,0,1:T(8,128)(2,1)} %bitcast.12), calls=%async_computation.1 | async-start | bytes 3145728 | tf_op jit(solution)/shard_map/all_to_all | solution.py:35
  63.3 279.0 %reduce-scatter.2.cloned.1.call-start = ((), (), s32[]{:S(2)}) async-start(), calls=%async_computation.4 | async-start | bytes 1769472 | tf_op jit(solution)/shard_map/reduce_scatter | solution.py:23
  63.4 6.7 %copy-start.1 = (bf16[192,3584]{1,0:T(8,128)(2,1)S(1)}, bf16[192,3584]{1,0:T(8,128)(2,1)}, u32[]{:S(2)}) copy-start(bf16[192,3584]{1,0:T(8,128)(2,1)} %copy-done) | copy-start | bytes 4128772
Sparse Core Ops, SparseCore 0:
  10.2 46.8 all-gather.7
  58.6 105.5 all-gather.3
  165.8 96.0 all-gather.5
  274.1 65.4 reduce-scatter.1
